TPU v7x, 128 devices: a whole 4x4x4 slice. The times are simulated.
128 devices in a mesh: gx: 8 (over x, core), gy: 16 (over z, y).
Axes of the slice: x: 4, y: 4, z: 4, core: 2. Of those that a mesh axis runs over, the one named last changes fastest.
Arguments:
- samples: bfloat16 [128, 256, 32, 256], P('gx', 'gy'), may hold values from -6 to 6
- leaf_basis: bfloat16 [64, 256], replicated, may hold values from -0.375 to 0.375
- transfer: bfloat16 [5, 64, 256], replicated, may hold values from -0.5 to 0.5
- coupling: bfloat16 [5, 7, 64, 448], replicated, may hold values from -0.15625 to 0.15625
- near_tiles: bfloat16 [9, 256, 256], replicated, may hold values from -0.125 to 0.125
- codes_local: int32 [128, 256, 4, 27], P('gx', 'gy'), may hold values from 0 to 35, as said below
- counts_local: int32 [128, 256, 4], P('gx', 'gy'), may hold values from 1 to 27, as said below
- codes_upper: int32 [168, 27], replicated, may hold values from 0 to 35, as said below
- counts_upper: int32 [168], replicated, may hold values from 1 to 27, as said below
Outputs:
- response: bfloat16 [128, 256, 32, 256], P('gx', 'gy')
Inputs may be any that keep to these rules, and one draw needn't show every extreme that they name: `codes_local`: entries [i, j, l, :] with i and j multiples of 2^l hold the list of the level-l cluster whose first leaf is (i, j); other entries are not read. Its first count entries are distinct codes a * 6 + b of clusters more than one step away from the target in some direction. `counts_local`: length of the list stored at the same position. `codes_upper`: row n is the list of the n-th cluster of level 4 and coarser, levels in order from 4, row-major within a level, each level with half the rows and columns of the one before and the last with 2 rows; first count entries distinct codes of clusters more than one step away from the target in some direction. `counts_upper`: length of the list of the same row.
All inputs are finite; a program needn't handle non-finite values.
Results may differ from a plain program's by a relative error of at most 0.0095.
Values may be sent and summed in bfloat16 or wider, within the bound.
No kernel may reach another device: no remote copies, remote signals or barrier semaphores. Data moves between devices by JAX's collectives and lax.ppermute only.
A program may use at most 384 MiB of HBM per device.

v0:
```python
import jax
import jax.numpy as jnp
from jax import lax
from jax.sharding import Mesh
from jax.sharding import PartitionSpec as P

GX_GY = ("gx_0", "gx_1", "gy_0", "gy_1")
GX = ("gx_0", "gx_1")
GY = ("gy_0", "gy_1")


def extended(block, sides, width):
    for axis, dim in sides:
        count = lax.axis_size(axis)
        forward = [(i, i + 1) for i in range(count - 1)]
        backward = [(target, source) for source, target in forward]
        low = lax.ppermute(
            lax.slice_in_dim(block, block.shape[dim] - width, None, axis=dim), axis, forward
        )
        high = lax.ppermute(lax.slice_in_dim(block, 0, width, axis=dim), axis, backward)
        block = jnp.concatenate([low, block, high], axis=dim)
    return block


def joined_along(blocks, dim):
    blocks = jnp.moveaxis(blocks, 0, dim)
    lengths = blocks.shape
    return blocks.reshape(*lengths[:dim], lengths[dim] * lengths[dim + 1], *lengths[dim + 2 :])


def stacked_from(value, axes, sequence):
    blocks = value[None]
    for k in sequence:
        blocks = lax.all_gather(blocks, axes[k], axis=0, tiled=True)
    current = [lax.axis_size(axes[k]) for k in reversed(sequence)]
    blocks = blocks.reshape(*current, *value.shape)
    turned = sorted(range(len(sequence)), key=lambda place: sequence[len(sequence) - 1 - place])
    return blocks.transpose(*turned, *range(len(sequence), blocks.ndim)).reshape(-1, *value.shape)


def gathered_by_axis(value, axes, sequence, dim):
    return joined_along(stacked_from(value, axes, sequence), dim)


def is_near(row_step, col_step):
    return abs(row_step) <= 1 and abs(col_step) <= 1


def project(leaf_samples, leaf_basis):
    coeffs = jnp.einsum(
        "ijvs,rs->ijvr", leaf_samples, leaf_basis, preferred_element_type=jnp.float32
    )
    return coeffs.astype(jnp.bfloat16)


def lift_level(children, matrices):
    grid_rows, grid_cols, vectors, rank_size = children.shape
    grouped = children.reshape(grid_rows // 2, 2, grid_cols // 2, 2, vectors, rank_size)
    grouped = grouped.transpose(0, 2, 4, 1, 3, 5).reshape(
        grid_rows // 2, grid_cols // 2, vectors, 4 * rank_size
    )
    parent = jnp.einsum("pqvc,sc->pqvs", grouped, matrices, preferred_element_type=jnp.float32)
    return parent.astype(jnp.bfloat16)


def spread(parent, matrices):
    grid_rows, grid_cols, vectors, rank_size = parent.shape
    carried = jnp.einsum("pqvs,sc->pqvc", parent, matrices, preferred_element_type=jnp.float32)
    carried = carried.reshape(grid_rows, grid_cols, vectors, 2, 2, rank_size).transpose(
        0, 3, 1, 4, 2, 5
    )
    return carried.reshape(2 * grid_rows, 2 * grid_cols, vectors, rank_size)


def member_table(list_codes, counts):
    slot_index = jnp.arange(list_codes.shape[-1], dtype=jnp.int32)
    active = slot_index < counts[..., None]
    matches = (list_codes[..., None] == jnp.arange(36, dtype=jnp.int32)) & active[..., None]
    return jnp.any(matches, axis=-2).astype(jnp.float32)


def couple(padded, member, matrices):
    grid_rows = padded.shape[0] - 4
    grid_cols = padded.shape[1] - 4
    vectors = padded.shape[2]
    rank_size = padded.shape[3]
    member = member.reshape(grid_rows // 2, 2, grid_cols // 2, 2, 36)
    totals = [
        [
            jnp.zeros((grid_rows // 2, grid_cols // 2, vectors, rank_size), jnp.float32)
            for col_bit in range(2)
        ]
        for row_bit in range(2)
    ]
    for code_row in range(6):
        for code_col in range(6):
            parities = [
                (row_bit, col_bit)
                for row_bit in range(2)
                for col_bit in range(2)
                if not is_near(code_row - 2 - row_bit, code_col - 2 - col_bit)
            ]
            if not parities:
                continue
            source = padded[
                code_row : code_row + grid_rows : 2, code_col : code_col + grid_cols : 2
            ]
            blocks = jnp.concatenate(
                [
                    matrices[
                        code_row + 1 - row_bit,
                        :,
                        (code_col + 1 - col_bit) * rank_size : (code_col + 2 - col_bit) * rank_size,
                    ]
                    for row_bit, col_bit in parities
                ],
                axis=0,
            )
            images = jnp.einsum("pqvr,sr->pqvs", source, blocks, preferred_element_type=jnp.float32)
            for number, (row_bit, col_bit) in enumerate(parities):
                weight_mask = member[:, row_bit, :, col_bit, code_row * 6 + code_col]
                totals[row_bit][col_bit] = (
                    totals[row_bit][col_bit]
                    + weight_mask[..., None, None]
                    * images[..., number * rank_size : (number + 1) * rank_size]
                )
    stacked = jnp.stack([jnp.stack(totals[row_bit], axis=0) for row_bit in range(2)], axis=0)
    return stacked.transpose(2, 0, 3, 1, 4, 5).reshape(grid_rows, grid_cols, vectors, rank_size)


def couple_one(padded, member, matrices, row_here, col_here):
    vectors = padded.shape[2]
    rank_size = padded.shape[3]
    window = lax.dynamic_slice(
        padded, (2 * (row_here // 2), 2 * (col_here // 2), 0, 0), (6, 6, vectors, rank_size)
    )
    row_bit = row_here % 2
    col_bit = col_here % 2
    summed = jnp.zeros((vectors, rank_size), jnp.float32)
    for code_row in range(6):
        for code_col in range(6):
            coupling_block = lax.dynamic_slice(
                matrices,
                (code_row + 1 - row_bit, 0, (code_col + 1 - col_bit) * rank_size),
                (1, rank_size, rank_size),
            )[0]
            term = jnp.einsum(
                "vr,sr->vs",
                window[code_row, code_col],
                coupling_block,
                preferred_element_type=jnp.float32,
            )
            summed = summed + member[code_row * 6 + code_col] * term
    return summed


def halo_coeffs(coeffs):
    grid_rows, grid_cols, vectors, rank_size = coeffs.shape
    flattened = coeffs.reshape(grid_rows, grid_cols, vectors * rank_size)
    padded = extended(flattened, ((GX, 0), (GY, 1)), 2)
    return padded.reshape(grid_rows + 4, grid_cols + 4, vectors, rank_size)


def shards(
    samples,
    leaf_basis,
    transfer,
    coupling,
    near_tiles,
    codes_local,
    counts_local,
    codes_upper,
    counts_upper,
):
    patch_size = samples.shape[0]
    vectors = samples.shape[2]
    rank_size = leaf_basis.shape[0]
    levels_local = transfer.shape[0] - 1
    images = []
    wide_samples = extended(samples, ((GX, 0), (GY, 1)), 2)
    first_padded = project(wide_samples, leaf_basis)
    leaf_coeffs = first_padded[2:-2, 2:-2]
    rim_samples = wide_samples[1:-1, 1:-1]
    coeffs = leaf_coeffs
    for level_index in range(levels_local):
        stride = 2**level_index
        member = member_table(
            codes_local[::stride, ::stride, level_index],
            counts_local[::stride, ::stride, level_index],
        )
        if level_index == 0 and first_padded is not None:
            padded = first_padded
        else:
            padded = halo_coeffs(coeffs)
        images.append(couple(padded, member, coupling[level_index]))
        coeffs = lift_level(coeffs, transfer[level_index])
    flat_block = coeffs.reshape(1, vectors * rank_size)
    everything = gathered_by_axis(flat_block, GX_GY, (0, 2, 3, 1), 0)
    block_grid = everything.reshape(lax.axis_size(GX), lax.axis_size(GY), vectors, rank_size)
    upper_coeffs = [block_grid]
    while upper_coeffs[-1].shape[0] > 2:
        upper_coeffs.append(lift_level(upper_coeffs[-1], transfer[levels_local]))
    row_index = lax.axis_index(GX)
    col_index = lax.axis_index(GY)
    offset = 0
    upper_images = []
    for upper_step, coeffs_here in enumerate(upper_coeffs):
        grid_cols = coeffs_here.shape[1]
        row_here = row_index // 2**upper_step
        col_here = col_index // 2**upper_step
        index_here = offset + row_here * grid_cols + col_here
        list_row = lax.dynamic_slice_in_dim(codes_upper, index_here, 1, 0)
        count_row = lax.dynamic_slice_in_dim(counts_upper, index_here, 1, 0)
        member = member_table(list_row, count_row)[0]
        padded = jnp.pad(coeffs_here, ((2, 2), (2, 2), (0, 0), (0, 0)))
        upper_images.append(couple_one(padded, member, coupling[levels_local], row_here, col_here))
        offset = offset + coeffs_here.shape[0] * grid_cols
    downward = upper_images[-1]
    for upper_step in range(len(upper_coeffs) - 2, -1, -1):
        row_here = row_index // 2**upper_step
        col_here = col_index // 2**upper_step
        child_slot = row_here % 2 * 2 + col_here % 2
        carried = jnp.einsum(
            "vs,sc->vc",
            downward.astype(jnp.bfloat16),
            transfer[levels_local],
            preferred_element_type=jnp.float32,
        )
        downward = upper_images[upper_step] + lax.dynamic_slice_in_dim(
            carried, child_slot * rank_size, rank_size, 1
        )
    downward = downward[None, None]
    for level_index in range(levels_local - 1, -1, -1):
        downward = images[level_index] + spread(
            downward.astype(jnp.bfloat16), transfer[level_index]
        )
    summed = jnp.einsum(
        "ijvr,rs->ijvs",
        downward.astype(jnp.bfloat16),
        leaf_basis,
        preferred_element_type=jnp.float32,
    )
    for step_row in range(3):
        for step_col in range(3):
            neighbour = rim_samples[
                step_row : step_row + patch_size, step_col : step_col + patch_size
            ]
            summed = summed + jnp.einsum(
                "ijvs,ts->ijvt",
                neighbour,
                near_tiles[step_row * 3 + step_col],
                preferred_element_type=jnp.float32,
            )
    return summed.astype(jnp.bfloat16)


def solution(mesh):
    torus = Mesh(mesh.devices.reshape(4, 2, 4, 4), ("gx_0", "gx_1", "gy_0", "gy_1"))
    in_specs = (
        P(GX, GY, None, None),
        P(),
        P(),
        P(),
        P(),
        P(GX, GY, None, None),
        P(GX, GY, None),
        P(),
        P(),
    )
    out_specs = P(GX, GY, None, None)
    return jax.shard_map(
        shards, mesh=torus, in_specs=in_specs, out_specs=out_specs, check_vma=False
    )
```

profile of v0, /device:TPU:38, one launch (start us, length us, event | category | flops | bytes accessed | tf_op | source)
XLA Modules:
  0.0 625.4 jit_solution(9527153466392710589)
XLA Ops:
  41.1 5.5 fusion.17
  53.1 3.7 slice_reduce_fusion.104
  60.5 3.7 slice_reduce_fusion.107
  78.8 6.7 %fusion.435 = f32[16,16,32,256]{3,2,1,0:T(8,128)} fusion(bf16[16,16,32,256]{3,2,1,0:T(8,128)(2,1)} %param.9, bf16[9,256,256]{2,1,0:T(8,128)(2,1)} %param.13), kind=kOutput, calls=%fused_computation.926 | convolution fusion | flops 1073741824 | bytes 12713984 | tf_op jit(solution)/shard_map/ijvs,ts->ijvt/dot_general | solution.py:248
  86.9 3.7 slice_reduce_fusion.106
  93.7 4.5 collective-permute-start.3
  100.2 5.4 fusion.10
  105.6 5.4 fusion.6
  111.2 6.2 collective-permute-done.2
  130.1 12.0 %all_gather.12 = bf16[4,1,2048]{2,1,0:T(2,128)(2,1)S(1)} all-gather(bf16[1,1,2048]{2,1,0:T(2,128)(2,1)S(1)} %broadcast_in_dim_reshape.3), channel_id=1, replica_groups=mesh['gx_0'=4,'gx_1'=2,'gy_0'=4,'gy_1'=4] {'gx_0'}, dimensions={0}, use_global_device_ids=true | all-gather | bytes 20480 | tf_op jit(solution)/shard_map/all_gather | solution.py:34
  142.1 13.2 %all_gather.13 = bf16[16,1,2048]{2,1,0:T(2,128)(2,1)S(1)} all-gather(bf16[4,1,2048]{2,1,0:T(2,128)(2,1)S(1)} %all_gather.12), channel_id=1, replica_groups=mesh['gx_0'=4,'gx_1'=2,'gy_0'=4,'gy_1'=4] {'gy_0'}, dimensions={0}, use_global_device_ids=true | all-gather | bytes 81920 | tf_op jit(solution)/shard_map/all_gather | solution.py:34
  155.3 12.3 %all_gather.14 = bf16[64,1,2048]{2,0,1:T(8,128)(2,1)S(1)} all-gather(bf16[16,1,2048]{2,0,1:T(8,128)(2,1)S(1)} %copy.124), channel_id=1, replica_groups=mesh['gx_0'=4,'gx_1'=2,'gy_0'=4,'gy_1'=4] {'gy_1'}, dimensions={0}, use_global_device_ids=true | all-gather | bytes 327680 | tf_op jit(solution)/shard_map/all_gather | solution.py:34
  341.3 15.0 %fusion.148 = f32[1,8,8,32,64]{4,3,2,1,0:T(8,128)} fusion(f32[8,8,32,256]{3,2,1,0:T(8,128)} %fusion.267, f32[8,8,32,256]{3,2,1,0:T(8,128)S(1)} %fusion.269, f32[8,8,32,256]{3,2,1,0:T(8,128)} %fusion.271, f32[8,8,32,256]{3,2,1,0:T(8,128)} %fusion.273, f32[8,8,32,256]{3,2,1,0:T(8,128)} %fusion.275, f32[8,8,32,256]{3,2,1,0:T(8,128)} %fusion.277, ...), kind=kLoop, calls=%fused_computation.411 | loop fusion | flops 6946816 | bytes 14686976 | tf_op jit(solution)/shard_map/stack | solution.py:127
  359.0 8.8 %fusion.175 = f32[1,8,8,32,64]{4,3,2,1,0:T(8,128)} fusion(f32[8,8,32,256]{3,2,1,0:T(8,128)S(1)} %copy-done.18, f32[8,8,32,256]{3,2,1,0:T(8,128)S(1)} %fusion.269, f32[8,8,32,256]{3,2,1,0:T(8,128)S(1)} %copy-done.5, f32[8,8,32,256]{3,2,1,0:T(8,128)S(1)} %copy-done.6, f32[8,8,32,256]{3,2,1,0:T(8,128)S(1)} %copy-done.7, f32[8,8,32,256]{3,2,1,0:T(8,128)S(1)} %copy-done.8, ...), kind=kLoop, calls=%fused_computation.465 | loop fusion | flops 6946816 | bytes 14686976 | tf_op jit(solution)/shard_map/stack | solution.py:127
  368.2 12.3 %fusion.202 = f32[1,8,8,32,64]{4,3,2,1,0:T(8,128)} fusion(f32[8,8,32,256]{3,2,1,0:T(8,128)S(1)} %copy-done.18, f32[8,8,32,256]{3,2,1,0:T(8,128)S(1)} %fusion.269, f32[8,8,32,256]{3,2,1,0:T(8,128)S(1)} %copy-done.5, f32[8,8,32,256]{3,2,1,0:T(8,128)S(1)} %copy-done.6, f32[8,8,32,256]{3,2,1,0:T(8,128)S(1)} %copy-done.7, f32[8,8,32,256]{3,2,1,0:T(8,128)S(1)} %copy-done.8, ...), kind=kLoop, calls=%fused_computation.519 | loop fusion | flops 6946816 | bytes 14686976 | tf_op jit(solution)/shard_map/stack | solution.py:127
  380.8 6.4 %fusion.229 = f32[1,8,8,32,64]{4,3,2,1,0:T(8,128)} fusion(f32[8,8,32,256]{3,2,1,0:T(8,128)S(1)} %copy-done.18, f32[8,8,32,256]{3,2,1,0:T(8,128)S(1)} %fusion.269, f32[8,8,32,256]{3,2,1,0:T(8,128)S(1)} %copy-done.5, f32[8,8,32,256]{3,2,1,0:T(8,128)S(1)} %copy-done.6, f32[8,8,32,256]{3,2,1,0:T(8,128)S(1)} %copy-done.7, f32[8,8,32,256]{3,2,1,0:T(8,128)S(1)} %copy-done.8, ...), kind=kLoop, calls=%fused_computation.573 | loop fusion | flops 6946816 | bytes 14686976 | tf_op jit(solution)/shard_map/stack | solution.py:127
  387.2 4.2 maximum_bitcast_fusion.1
  393.2 6.8 %fusion.25 = f32[16,16,32,256]{3,2,1,0:T(8,128)} fusion(bf16[20,16,32,256]{3,2,1,0:T(8,128)(2,1)} %copy-done.1, bf16[20,2,32,256]{3,2,1,0:T(8,128)(2,1)} %copy-done.28, bf16[9,256,256]{2,1,0:T(8,128)(2,1)} %param.13), kind=kOutput, calls=%fused_computation.138 | convolution fusion | flops 1085538304 | bytes 14417920 | tf_op jit(solution)/shard_map/ijvs,ts->ijvt/dot_general | solution.py:248
  400.0 6.7 %fusion.24 = f32[16,16,32,256]{3,2,1,0:T(8,128)} fusion(bf16[20,16,32,256]{3,2,1,0:T(8,128)(2,1)} %copy-done.1, bf16[20,2,32,256]{3,2,1,0:T(8,128)(2,1)S(1)} %copy-done.29, bf16[9,256,256]{2,1,0:T(8,128)(2,1)} %param.13), kind=kOutput, calls=%fused_computation.137 | convolution fusion | flops 1085538304 | bytes 14417920 | tf_op jit(solution)/shard_map/ijvs,ts->ijvt/dot_general | solution.py:248
  406.7 5.5 fusion.26
  412.2 5.4 fusion.22
  417.5 5.4 fusion.23
  426.7 3.8 collective-permute-start.13
  440.4 3.9 collective-permute-start.14
  447.9 6.0 collective-permute-start.11
  458.5 6.2 collective-permute-start.7
  474.9 17.4 %fusion.1578 = f32[1,1,1,32,64]{4,3,0,2,1:T(8,128)S(1)} fusion(f32[1,1,32,256]{3,2,1,0:T(8,128)S(1)} %convolution_bitcast_fusion.4, f32[1,1,32,256]{3,2,1,0:T(8,128)S(1)} %convolution_bitcast_fusion.5, f32[1,1,32,256]{3,2,1,0:T(8,128)S(1)} %convolution_bitcast_fusion.6, f32[1,1,32,256]{3,2,1,0:T(8,128)S(1)} %convolution_bitcast_fusion.7, ...), kind=kLoop, calls=%fused_computation.2436 | loop fusion | flops 108544 | bytes 229484 | tf_op jit(solution)/shard_map/stack | solution.py:127
  492.3 17.0 %fusion.1605 = f32[1,1,1,32,64]{4,3,0,2,1:T(8,128)S(1)} fusion(f32[1,1,32,256]{3,2,1,0:T(8,128)S(1)} %convolution_bitcast_fusion.4, f32[1,1,32,256]{3,2,1,0:T(8,128)S(1)} %convolution_bitcast_fusion.5, f32[1,1,32,256]{3,2,1,0:T(8,128)S(1)} %convolution_bitcast_fusion.6, f32[1,1,32,256]{3,2,1,0:T(8,128)S(1)} %convolution_bitcast_fusion.7, ...), kind=kLoop, calls=%fused_computation.2490 | loop fusion | flops 108544 | bytes 229484 | tf_op jit(solution)/shard_map/stack | solution.py:127
  509.9 16.7 %fusion.1551 = f32[1,1,1,32,64]{4,3,2,1,0:T(8,128)S(1)} fusion(f32[1,1,32,256]{3,2,1,0:T(8,128)S(1)} %convolution_bitcast_fusion.4, f32[1,1,32,256]{3,2,1,0:T(8,128)S(1)} %convolution_bitcast_fusion.5, f32[1,1,32,256]{3,2,1,0:T(8,128)S(1)} %convolution_bitcast_fusion.6, f32[1,1,32,256]{3,2,1,0:T(8,128)S(1)} %convolution_bitcast_fusion.7, ...), kind=kLoop, calls=%fused_computation.2382 | loop fusion | flops 108544 | bytes 229484 | tf_op jit(solution)/shard_map/stack | solution.py:127
  526.7 17.0 %fusion.1524 = f32[1,1,1,32,64]{4,3,2,1,0:T(8,128)S(1)} fusion(f32[1,1,32,256]{3,2,1,0:T(8,128)S(1)} %convolution_bitcast_fusion.4, f32[1,1,32,256]{3,2,1,0:T(8,128)S(1)} %convolution_bitcast_fusion.5, f32[1,1,32,256]{3,2,1,0:T(8,128)S(1)} %convolution_bitcast_fusion.6, f32[1,1,32,256]{3,2,1,0:T(8,128)S(1)} %convolution_bitcast_fusion.7, ...), kind=kLoop, calls=%fused_computation.2328 | loop fusion | flops 108544 | bytes 229484 | tf_op jit(solution)/shard_map/stack | solution.py:127
  594.2 4.4 fusion.1246
  598.7 26.5 %add_convert_fusion = bf16[16,16,32,256]{3,2,1,0:T(8,128)(2,1)} fusion(f32[16,16,32,256]{3,2,1,0:T(8,128)} %fusion.10, f32[16,16,32,256]{3,2,1,0:T(8,128)} %fusion.24, f32[16,16,32,256]{3,2,1,0:T(8,128)} %fusion.22, f32[16,16,32,256]{3,2,1,0:T(8,128)} %fusion.435, f32[16,16,32,256]{3,2,1,0:T(8,128)} %fusion.25, f32[16,16,32,256]{3,2,1,0:T(8,128)} %fusion.23, ...), kind=kOutput, calls=%fused_computation.36 | convolution fusion | flops 1106509824 | bytes 85721088 | tf_op jit(solution)/shard_map/ijvs,ts->ijvt/dot_general | solution.py:248
  (1179 shorter events, 341.2 us)
Async XLA Ops:
  0.0 117.4 %copy-start = (bf16[64,256]{1,0:T(8,128)(2,1)S(1)}, bf16[64,256]{1,0:T(8,128)(2,1)}, u32[]{:S(2)}) copy-start(bf16[64,256]{1,0:T(8,128)(2,1)} %param.10) | copy-start | bytes 98308
  2.3 88.2 %collective-permute-start = (bf16[2,16,32,256]{3,2,1,0:T(8,128)(2,1)}, bf16[2,16,32,256]{3,2,1,0:T(8,128)(2,1)S(1)}, u32[]{:S(2)}, u32[]{:S(2)}) collective-permute-start(bf16[2,16,32,256]{3,2,1,0:T(8,128)(2,1)} %get-tuple-element.334), channel_id=1, source_target_pairs={{0,16},{16,32},{32,48},{48,64},{64,80},{80,96},{96,112},{1,17},{17... | collective-permute-start | bytes 1572872 | tf_op jit(solution)/shard_map/ppermute | solution.py:17
  4.4 89.2 %collective-permute-start.1 = (bf16[2,16,32,256]{3,2,1,0:T(8,128)(2,1)}, bf16[2,16,32,256]{3,2,1,0:T(8,128)(2,1)S(1)}, u32[]{:S(2)}, u32[]{:S(2)}) collective-permute-start(bf16[2,16,32,256]{3,2,1,0:T(8,128)(2,1)} %get-tuple-element.335), channel_id=1, source_target_pairs={{16,0},{32,16},{48,32},{64,48},{80,64},{96,80},{112,96},{17,1},{33... | collective-permute-start | bytes 1572872 | tf_op jit(solution)/shard_map/ppermute | solution.py:20
  93.7 17.4 %collective-permute-start.3 = (bf16[20,2,32,256]{3,2,1,0:T(8,128)(2,1)S(1)}, bf16[20,2,32,256]{3,2,1,0:T(8,128)(2,1)S(1)}, u32[]{:S(2)}, u32[]{:S(2)}) collective-permute-start(bf16[20,2,32,256]{3,2,1,0:T(8,128)(2,1)S(1)} %get-tuple-element.332), channel_id=1, source_target_pairs={{1,0},{2,1},{3,2},{4,3},{5,4},{6,5},{7,6},{8,7},{9,8},{10,9},{11,1... | collective-permute-start | bytes 1966088 | tf_op jit(solution)/shard_map/ppermute | solution.py:20
  98.2 19.2 %collective-permute-start.2 = (bf16[20,2,32,256]{3,2,1,0:T(8,128)(2,1)S(1)}, bf16[20,2,32,256]{3,2,1,0:T(8,128)(2,1)S(1)}, u32[]{:S(2)}, u32[]{:S(2)}) collective-permute-start(bf16[20,2,32,256]{3,2,1,0:T(8,128)(2,1)S(1)} %get-tuple-element.333), channel_id=1, source_target_pairs={{0,1},{1,2},{2,3},{3,4},{4,5},{5,6},{6,7},{7,8},{8,9},{9,10},{10,1... | collective-permute-start | bytes 1966088 | tf_op jit(solution)/shard_map/ppermute | solution.py:17
  230.5 217.3 %collective-permute-start.4 = (bf16[2,8,2048]{2,1,0:T(8,128)(2,1)}, bf16[2,8,2048]{2,1,0:T(8,128)(2,1)}, u32[]{:S(2)}, u32[]{:S(2)}) collective-permute-start(bf16[2,8,2048]{2,1,0:T(8,128)(2,1)} %slice.5004), channel_id=1, source_target_pairs={{0,16},{16,32},{32,48},{48,64},{64,80},{80,96},{96,112},{1,17},{17... | collective-permute-start | bytes 196616 | tf_op jit(solution)/shard_map/ppermute | solution.py:17
  232.6 200.8 %collective-permute-start.12 = (bf16[2,2,2048]{2,1,0:T(2,128)(2,1)}, bf16[2,2,2048]{2,1,0:T(2,128)(2,1)}, u32[]{:S(2)}, u32[]{:S(2)}) collective-permute-start(bf16[2,2,2048]{2,1,0:T(2,128)(2,1)} %reshape.1625), channel_id=1, source_target_pairs={{0,16},{16,32},{32,48},{48,64},{64,80},{80,96},{96,112},{1,17},{17... | collective-permute-start | bytes 49160 | tf_op jit(solution)/shard_map/ppermute | solution.py:17
  235.2 205.2 %collective-permute-start.8 = (bf16[2,4,2048]{2,1,0:T(4,128)(2,1)}, bf16[2,4,2048]{2,1,0:T(4,128)(2,1)}, u32[]{:S(2)}, u32[]{:S(2)}) collective-permute-start(bf16[2,4,2048]{2,1,0:T(4,128)(2,1)} %slice.5302), channel_id=1, source_target_pairs={{0,16},{16,32},{32,48},{48,64},{64,80},{80,96},{96,112},{1,17},{17... | collective-permute-start | bytes 98312 | tf_op jit(solution)/shard_map/ppermute | solution.py:17
  426.7 11.7 %collective-permute-start.13 = (bf16[2,2,2048]{2,1,0:T(2,128)(2,1)}, bf16[2,2,2048]{2,1,0:T(2,128)(2,1)S(1)}, u32[]{:S(2)}, u32[]{:S(2)}) collective-permute-start(bf16[2,2,2048]{2,1,0:T(2,128)(2,1)} %reshape.1625), channel_id=1, source_target_pairs={{16,0},{32,16},{48,32},{64,48},{80,64},{96,80},{112,96},{17,1},{33... | collective-permute-start | bytes 49160 | tf_op jit(solution)/shard_map/ppermute | solution.py:20
  430.8 24.1 %collective-permute-start.5 = (bf16[2,8,2048]{2,1,0:T(8,128)(2,1)S(1)}, bf16[2,8,2048]{2,1,0:T(8,128)(2,1)S(1)}, u32[]{:S(2)}, u32[]{:S(2)}) collective-permute-start(bf16[2,8,2048]{2,1,0:T(8,128)(2,1)S(1)} %slice.5006), channel_id=1, source_target_pairs={{16,0},{32,16},{48,32},{64,48},{80,64},{96,80},{112,96},{17,1},{33... | collective-permute-start | bytes 196616 | tf_op jit(solution)/shard_map/ppermute | solution.py:20
  433.4 11.7 %collective-permute-start.9 = (bf16[2,4,2048]{2,1,0:T(4,128)(2,1)S(1)}, bf16[2,4,2048]{2,1,0:T(4,128)(2,1)S(1)}, u32[]{:S(2)}, u32[]{:S(2)}) collective-permute-start(bf16[2,4,2048]{2,1,0:T(4,128)(2,1)S(1)} %slice.5304), channel_id=1, source_target_pairs={{16,0},{32,16},{48,32},{64,48},{80,64},{96,80},{112,96},{17,1},{33... | collective-permute-start | bytes 98312 | tf_op jit(solution)/shard_map/ppermute | solution.py:20
  438.5 20.0 %collective-permute-start.15 = (bf16[6,2,2048]{2,1,0:T(2,128)(2,1)S(1)}, bf16[6,2,2048]{2,1,0:T(2,128)(2,1)S(1)}, u32[]{:S(2)}, u32[]{:S(2)}) collective-permute-start(bf16[6,2,2048]{2,1,0:T(2,128)(2,1)S(1)} %constant_dynamic-update-slice_fusion.9), channel_id=1, source_target_pairs={{1,0},{2,1},{3,2},{4,3},{5,4},{6,5},{7,6},{8,7},{9,8},{10,9},{11,1... | collective-permute-start | bytes 147464 | tf_op jit(solution)/shard_map/ppermute | solution.py:20
  440.4 24.3 %collective-permute-start.14 = (bf16[6,2,2048]{2,1,0:T(2,128)(2,1)S(1)}, bf16[6,2,2048]{2,1,0:T(2,128)(2,1)S(1)}, u32[]{:S(2)}, u32[]{:S(2)}) collective-permute-start(bf16[6,2,2048]{2,1,0:T(2,128)(2,1)S(1)} %constant_dynamic-update-slice_fusion.9), channel_id=1, source_target_pairs={{0,1},{1,2},{2,3},{3,4},{4,5},{5,6},{6,7},{7,8},{8,9},{9,10},{10,1... | collective-permute-start | bytes 147464 | tf_op jit(solution)/shard_map/ppermute | solution.py:17
  446.0 98.3 %collective-permute-start.10 = (bf16[8,2,2048]{2,1,0:T(2,128)(2,1)}, bf16[8,2,2048]{2,1,0:T(2,128)(2,1)}, u32[]{:S(2)}, u32[]{:S(2)}) collective-permute-start(bf16[8,2,2048]{2,1,0:T(2,128)(2,1)} %get-tuple-element.509), channel_id=1, source_target_pairs={{0,1},{1,2},{2,3},{3,4},{4,5},{5,6},{6,7},{7,8},{8,9},{9,10},{10,1... | collective-permute-start | bytes 196616 | tf_op jit(solution)/shard_map/ppermute | solution.py:17
  447.9 96.4 %collective-permute-start.11 = (bf16[8,2,2048]{2,1,0:T(2,128)(2,1)}, bf16[8,2,2048]{2,1,0:T(2,128)(2,1)}, u32[]{:S(2)}, u32[]{:S(2)}) collective-permute-start(bf16[8,2,2048]{2,1,0:T(2,128)(2,1)} %get-tuple-element.510), channel_id=1, source_target_pairs={{1,0},{2,1},{3,2},{4,3},{5,4},{6,5},{7,6},{8,7},{9,8},{10,9},{11,1... | collective-permute-start | bytes 196616 | tf_op jit(solution)/shard_map/ppermute | solution.py:20
  456.5 106.2 %collective-permute-start.6 = (bf16[12,2,2048]{2,1,0:T(2,128)(2,1)}, bf16[12,2,2048]{2,1,0:T(2,128)(2,1)}, u32[]{:S(2)}, u32[]{:S(2)}) collective-permute-start(bf16[12,2,2048]{2,1,0:T(2,128)(2,1)} %get-tuple-element.503), channel_id=1, source_target_pairs={{0,1},{1,2},{2,3},{3,4},{4,5},{5,6},{6,7},{7,8},{8,9},{9,10},{10,1... | collective-permute-start | bytes 294920 | tf_op jit(solution)/shard_map/ppermute | solution.py:17
  458.5 104.1 %collective-permute-start.7 = (bf16[12,2,2048]{2,1,0:T(2,128)(2,1)}, bf16[12,2,2048]{2,1,0:T(2,128)(2,1)}, u32[]{:S(2)}, u32[]{:S(2)}) collective-permute-start(bf16[12,2,2048]{2,1,0:T(2,128)(2,1)} %get-tuple-element.504), channel_id=1, source_target_pairs={{1,0},{2,1},{3,2},{4,3},{5,4},{6,5},{7,6},{8,7},{9,8},{10,9},{11,1... | collective-permute-start | bytes 294920 | tf_op jit(solution)/shard_map/ppermute | solution.py:20
  474.5 71.5 %copy-start.67 = (bf16[64,64]{0,1:T(8,128)(2,1)S(1)}, bf16[64,64]{0,1:T(8,128)(2,1)}, u32[]{:S(2)}) copy-start(bf16[64,64]{0,1:T(8,128)(2,1)} %get-tuple-element.414) | copy-start | bytes 24580
  474.5 71.5 %copy-start.68 = (bf16[64,64]{0,1:T(8,128)(2,1)S(1)}, bf16[64,64]{0,1:T(8,128)(2,1)}, u32[]{:S(2)}) copy-start(bf16[64,64]{0,1:T(8,128)(2,1)} %get-tuple-element.416) | copy-start | bytes 24580
  474.7 71.5 %copy-start.69 = (bf16[64,64]{0,1:T(8,128)(2,1)S(1)}, bf16[64,64]{0,1:T(8,128)(2,1)}, u32[]{:S(2)}) copy-start(bf16[64,64]{0,1:T(8,128)(2,1)} %get-tuple-element.418) | copy-start | bytes 24580
  474.7 71.7 %copy-start.73 = (bf16[64,64]{0,1:T(8,128)(2,1)S(1)}, bf16[64,64]{0,1:T(8,128)(2,1)}, u32[]{:S(2)}) copy-start(bf16[64,64]{0,1:T(8,128)(2,1)} %get-tuple-element.404) | copy-start | bytes 24580
  474.7 71.7 %copy-start.76 = (bf16[64,64]{0,1:T(8,128)(2,1)S(1)}, bf16[64,64]{0,1:T(8,128)(2,1)}, u32[]{:S(2)}) copy-start(bf16[64,64]{0,1:T(8,128)(2,1)} %get-tuple-element.399) | copy-start | bytes 24580
  474.8 71.8 %copy-start.71 = (bf16[64,64]{0,1:T(8,128)(2,1)S(1)}, bf16[64,64]{0,1:T(8,128)(2,1)}, u32[]{:S(2)}) copy-start(bf16[64,64]{0,1:T(8,128)(2,1)} %get-tuple-element.408) | copy-start | bytes 24580
  474.8 72.0 %copy-start.78 = (bf16[64,64]{0,1:T(8,128)(2,1)S(1)}, bf16[64,64]{0,1:T(8,128)(2,1)}, u32[]{:S(2)}) copy-start(bf16[64,64]{0,1:T(8,128)(2,1)} %get-tuple-element.392) | copy-start | bytes 24580
  474.8 72.0 %copy-start.79 = (bf16[64,64]{0,1:T(8,128)(2,1)S(1)}, bf16[64,64]{0,1:T(8,128)(2,1)}, u32[]{:S(2)}) copy-start(bf16[64,64]{0,1:T(8,128)(2,1)} %get-tuple-element.391) | copy-start | bytes 24580
  474.8 72.2 %copy-start.77 = (bf16[64,64]{0,1:T(8,128)(2,1)S(1)}, bf16[64,64]{0,1:T(8,128)(2,1)}, u32[]{:S(2)}) copy-start(bf16[64,64]{0,1:T(8,128)(2,1)} %get-tuple-element.393) | copy-start | bytes 24580
  492.2 55.0 %copy-start.66 = (bf16[64,64]{0,1:T(8,128)(2,1)S(1)}, bf16[64,64]{0,1:T(8,128)(2,1)}, u32[]{:S(2)}) copy-start(bf16[64,64]{0,1:T(8,128)(2,1)} %get-tuple-element.402) | copy-start | bytes 24580
  492.2 55.0 %copy-start.74 = (bf16[64,64]{0,1:T(8,128)(2,1)S(1)}, bf16[64,64]{0,1:T(8,128)(2,1)}, u32[]{:S(2)}) copy-start(bf16[64,64]{0,1:T(8,128)(2,1)} %get-tuple-element.397) | copy-start | bytes 24580
  492.2 55.2 %copy-start.65 = (bf16[64,64]{0,1:T(8,128)(2,1)S(1)}, bf16[64,64]{0,1:T(8,128)(2,1)}, u32[]{:S(2)}) copy-start(bf16[64,64]{0,1:T(8,128)(2,1)} %get-tuple-element.406) | copy-start | bytes 24580
  492.3 55.5 %copy-start.59 = (bf16[64,64]{0,1:T(8,128)(2,1)S(1)}, bf16[64,64]{0,1:T(8,128)(2,1)}, u32[]{:S(2)}) copy-start(bf16[64,64]{0,1:T(8,128)(2,1)} %get-tuple-element.390) | copy-start | bytes 24580
  492.3 55.7 %copy-start.130 = (bf16[64,64]{0,1:T(8,128)(2,1)S(1)}, bf16[64,64]{0,1:T(8,128)(2,1)}, u32[]{:S(2)}) copy-start(bf16[64,64]{0,1:T(8,128)(2,1)} %get-tuple-element.383) | copy-start | bytes 24580
  492.3 55.7 %copy-start.136 = (bf16[64,64]{0,1:T(8,128)(2,1)S(1)}, bf16[64,64]{0,1:T(8,128)(2,1)}, u32[]{:S(2)}) copy-start(bf16[64,64]{0,1:T(8,128)(2,1)} %get-tuple-element.384) | copy-start | bytes 24580
  (364 other events, 2996.3 us)
where the time goes:
time: 637 us; the launch traced here: 625 us
  matrix products  268 us (42%)
  other arithmetic  143 us (22%)
  local copies, waits for them, and re-layouts  112 us (18%)
  starting transfers between devices  49.8 us (8%)
  blocking collectives  39.7 us (6%)
  between operations  6.47 us (1%)
  waiting for transfers between devices  6.44 us (1%)
    another operation x16, other arithmetic, couple(): jnp.stack(totals[row_bit], axis=0)  125 us
    dot_general x106, matrix products, couple_one(): jnp.einsum('vr,sr->vs', window[code_row, code_col], coupling_block, prefe...  92.1 us
    dot_general x128, matrix products, couple(): jnp.einsum('pqvr,sr->pqvs', source, blocks, preferred_element_type=jnp.fl...  86.4 us
    dot_general x9, matrix products, shards(): jnp.einsum('ijvs,ts->ijvt', neighbour, near_tiles[step_row * 3 + step_col...  73.8 us
    all_gather x4, blocking collectives, stacked_from(): blocks = lax.all_gather(blocks, axes[k], axis=0, tiled=True)  39.7 us
    slice x24, local copies, waits for them, and re-layouts, couple(): weight_mask = member[:, row_bit, :, col_bit, code_row * 6 + code_col]  39.4 us
    ppermute x8, starting transfers between devices, extended(): lax.ppermute(lax.slice_in_dim(block, 0, width, axis=dim), axis, backward)  32.1 us
    ppermute x8, starting transfers between devices, extended(): lax.ppermute(lax.slice_in_dim(block, block.shape[dim] - width, None, axis...  17.7 us
  transfers between devices with their start and end apart: 16, of which 2 were waited for; matrix products, arithmetic and copies ran while one was open for 61% of the time, Pallas kernels for 0%

commit v1 on v0

--- a/solution.py
+++ b/solution.py
@@ -31,7 +31,9 @@
 def stacked_from(value, axes, sequence):
     blocks = value[None]
     for k in sequence:
-        blocks = lax.all_gather(blocks, axes[k], axis=0, tiled=True)
+        blocks = jnp.concatenate(
+            lax.all_to_all(jnp.stack([blocks] * lax.axis_size(axes[k])), axes[k], 0, 0), axis=0
+        )
     current = [lax.axis_size(axes[k]) for k in reversed(sequence)]
     blocks = blocks.reshape(*current, *value.shape)
     turned = sorted(range(len(sequence)), key=lambda place: sequence[len(sequence) - 1 - place])

time: 637 us -> 587 us (0.922)
  blocking collectives: 39.7 us -> 4.15 us
  matrix products: 268 us -> 252 us
  starting transfers between devices: 49.8 us -> 65.3 us
  local copies, waits for them, and re-layouts: 112 us -> 105 us
    all_gather x4 -> x0, blocking collectives: 39.7 us -> none  [stacked_from(): blocks = lax.all_gather(blocks, axes[k], axis=0, tiled=True)]
    all_to_all x0 -> x3, starting transfers between devices: none -> 18.1 us  [stacked_from(): lax.all_to_all(jnp.stack([blocks] * lax.axis_size(axes[k])), axes[k], 0, 0)]
    dot_general x128, matrix products: 86.4 us -> 72.9 us  [couple(): jnp.einsum('pqvr,sr->pqvs', source, blocks, preferred_element_type=jnp.fl...]
    unnamed x769 -> x718, local copies, waits for them, and re-layouts: 15.3 us -> 12.8 us
  transfers between devices with their start and end apart: 16 -> 19, of which waited for: 2 -> 2; matrix products, arithmetic and copies ran while one was open for 61% -> 49% of each run, Pallas kernels for 0% -> 0%
where the time goes in v1:
time: 587 us; the launch traced here: 576 us
  matrix products  252 us (43%)
  other arithmetic  138 us (24%)
  local copies, waits for them, and re-layouts  105 us (18%)
  starting transfers between devices  65.3 us (11%)
  between operations  6.61 us (1%)
  waiting for transfers between devices  6.46 us (1%)
    another operation x16, other arithmetic, couple(): jnp.stack(totals[row_bit], axis=0)  124 us
    dot_general x106, matrix products, couple_one(): jnp.einsum('vr,sr->vs', window[code_row, code_col], coupling_block, prefe...  88.8 us
    dot_general x128, matrix products, couple(): jnp.einsum('pqvr,sr->pqvs', source, blocks, preferred_element_type=jnp.fl...  72.9 us
    dot_general x9, matrix products, shards(): jnp.einsum('ijvs,ts->ijvt', neighbour, near_tiles[step_row * 3 + step_col...  71.4 us
    slice x24, local copies, waits for them, and re-layouts, couple(): weight_mask = member[:, row_bit, :, col_bit, code_row * 6 + code_col]  39.4 us
    ppermute x8, starting transfers between devices, extended(): lax.ppermute(lax.slice_in_dim(block, 0, width, axis=dim), axis, backward)  29.6 us
    all_to_all x3, starting transfers between devices, stacked_from(): lax.all_to_all(jnp.stack([blocks] * lax.axis_size(axes[k])), axes[k], 0, 0)  18.1 us
    ppermute x8, starting transfers between devices, extended(): lax.ppermute(lax.slice_in_dim(block, block.shape[dim] - width, None, axis...  17.6 us
  transfers between devices with their start and end apart: 19, of which 2 were waited for; matrix products, arithmetic and copies ran while one was open for 49% of the time, Pallas kernels for 0%

profile of v1, /device:TPU:38, one launch (start us, length us, event | category | flops | bytes accessed | tf_op | source)
XLA Modules:
  0.0 576.3 jit_solution(12899410287417693661)
XLA Ops:
  41.9 3.7 slice_reduce_fusion.103
  45.6 3.7 slice_reduce_fusion.104
  53.0 3.7 slice_reduce_fusion.107
  70.9 6.7 %fusion.435 = f32[16,16,32,256]{3,2,1,0:T(8,128)} fusion(bf16[16,16,32,256]{3,2,1,0:T(8,128)(2,1)} %param.9, bf16[9,256,256]{2,1,0:T(8,128)(2,1)} %param.13), kind=kOutput, calls=%fused_computation.928 | convolution fusion | flops 1073741824 | bytes 12713984 | tf_op jit(solution)/shard_map/ijvs,ts->ijvt/dot_general | solution.py:250
  79.0 3.7 slice_reduce_fusion.106
  85.9 4.5 collective-permute-start.3
  92.3 5.4 fusion.10
  97.7 5.4 fusion.6
  103.3 6.2 %collective-permute-done.2 = bf16[20,2,32,256]{3,2,1,0:T(8,128)(2,1)S(1)} collective-permute-done((bf16[20,2,32,256]{3,2,1,0:T(8,128)(2,1)S(1)}, bf16[20,2,32,256]{3,2,1,0:T(8,128)(2,1)S(1)}, u32[]{:S(2)}, u32[]{:S(2)}) %collective-permute-start.2) | collective-permute-done | bytes 655392 | tf_op jit(solution)/shard_map/ppermute | solution.py:17
  168.9 5.4 reshape.1625
  190.4 6.9 %all-to-all-start = ((bf16[4,2,1024]{2,1,0:T(2,128)(2,1)}), bf16[4,2,1024]{2,1,0:T(2,128)(2,1)S(1)}, u32[]{:S(2)}, u32[]{:S(2)}) async-start(bf16[4,2,1024]{2,1,0:T(2,128)(2,1)} %reshape.2124), calls=%async_computation | async-start | bytes 32768 | tf_op jit(solution)/shard_map/all_to_all | solution.py:35
  201.2 15.0 %fusion.148 = f32[1,8,8,32,64]{4,3,2,1,0:T(8,128)} fusion(f32[8,8,32,256]{3,2,1,0:T(8,128)} %fusion.267, f32[8,8,32,256]{3,2,1,0:T(8,128)S(1)} %fusion.269, f32[8,8,32,256]{3,2,1,0:T(8,128)} %fusion.271, f32[8,8,32,256]{3,2,1,0:T(8,128)} %fusion.273, f32[8,8,32,256]{3,2,1,0:T(8,128)} %fusion.275, f32[8,8,32,256]{3,2,1,0:T(8,128)} %fusion.277, ...), kind=kLoop, calls=%fused_computation.411 | loop fusion | flops 6946816 | bytes 14686976 | tf_op jit(solution)/shard_map/stack | solution.py:129
  218.9 8.2 %fusion.175 = f32[1,8,8,32,64]{4,3,2,1,0:T(8,128)} fusion(f32[8,8,32,256]{3,2,1,0:T(8,128)S(1)} %copy-done.16, f32[8,8,32,256]{3,2,1,0:T(8,128)S(1)} %fusion.269, f32[8,8,32,256]{3,2,1,0:T(8,128)S(1)} %copy-done.3, f32[8,8,32,256]{3,2,1,0:T(8,128)S(1)} %copy-done.4, f32[8,8,32,256]{3,2,1,0:T(8,128)S(1)} %copy-done.5, f32[8,8,32,256]{3,2,1,0:T(8,128)S(1)} %copy-done.6, ...), kind=kLoop, calls=%fused_computation.465 | loop fusion | flops 6946816 | bytes 14686976 | tf_op jit(solution)/shard_map/stack | solution.py:129
  227.4 12.3 %fusion.202 = f32[1,8,8,32,64]{4,3,2,1,0:T(8,128)} fusion(f32[8,8,32,256]{3,2,1,0:T(8,128)S(1)} %copy-done.16, f32[8,8,32,256]{3,2,1,0:T(8,128)S(1)} %fusion.269, f32[8,8,32,256]{3,2,1,0:T(8,128)S(1)} %copy-done.3, f32[8,8,32,256]{3,2,1,0:T(8,128)S(1)} %copy-done.4, f32[8,8,32,256]{3,2,1,0:T(8,128)S(1)} %copy-done.5, f32[8,8,32,256]{3,2,1,0:T(8,128)S(1)} %copy-done.6, ...), kind=kLoop, calls=%fused_computation.519 | loop fusion | flops 6946816 | bytes 14686976 | tf_op jit(solution)/shard_map/stack | solution.py:129
  240.0 7.4 %fusion.229 = f32[1,8,8,32,64]{4,3,2,1,0:T(8,128)} fusion(f32[8,8,32,256]{3,2,1,0:T(8,128)S(1)} %copy-done.16, f32[8,8,32,256]{3,2,1,0:T(8,128)S(1)} %fusion.269, f32[8,8,32,256]{3,2,1,0:T(8,128)S(1)} %copy-done.3, f32[8,8,32,256]{3,2,1,0:T(8,128)S(1)} %copy-done.4, f32[8,8,32,256]{3,2,1,0:T(8,128)S(1)} %copy-done.5, f32[8,8,32,256]{3,2,1,0:T(8,128)S(1)} %copy-done.6, ...), kind=kLoop, calls=%fused_computation.573 | loop fusion | flops 6946816 | bytes 14686976 | tf_op jit(solution)/shard_map/stack | solution.py:129
  247.5 5.5 fusion.25
  253.0 5.4 fusion.24
  258.4 5.5 fusion.26
  263.9 5.4 fusion.22
  269.2 5.6 fusion.23
  284.8 5.7 all-to-all-start.1
  296.4 3.9 collective-permute-start.14
  304.0 5.5 all-to-all-start.2
  309.5 5.3 collective-permute-start.11
  318.6 6.2 %collective-permute-start.7 = (bf16[12,2,2048]{2,1,0:T(2,128)(2,1)}, bf16[12,2,2048]{2,1,0:T(2,128)(2,1)}, u32[]{:S(2)}, u32[]{:S(2)}) collective-permute-start(bf16[12,2,2048]{2,1,0:T(2,128)(2,1)} %get-tuple-element.504), channel_id=1, source_target_pairs={{1,0},{2,1},{3,2},{4,3},{5,4},{6,5},{7,6},{8,7},{9,8},{10,9},{11,1... | collective-permute-start | bytes 294920 | tf_op jit(solution)/shard_map/ppermute | solution.py:20
  330.6 16.5 %fusion.1578 = f32[1,1,1,32,64]{4,3,0,2,1:T(8,128)S(1)} fusion(f32[1,1,32,256]{3,2,1,0:T(8,128)S(1)} %convolution_bitcast_fusion.4, f32[1,1,32,256]{3,2,1,0:T(8,128)S(1)} %convolution_bitcast_fusion.5, f32[1,1,32,256]{3,2,1,0:T(8,128)S(1)} %convolution_bitcast_fusion.6, f32[1,1,32,256]{3,2,1,0:T(8,128)S(1)} %convolution_bitcast_fusion.7, ...), kind=kLoop, calls=%fused_computation.2438 | loop fusion | flops 108544 | bytes 229484 | tf_op jit(solution)/shard_map/stack | solution.py:129
  347.1 17.1 %fusion.1605 = f32[1,1,1,32,64]{4,3,0,2,1:T(8,128)S(1)} fusion(f32[1,1,32,256]{3,2,1,0:T(8,128)S(1)} %convolution_bitcast_fusion.4, f32[1,1,32,256]{3,2,1,0:T(8,128)S(1)} %convolution_bitcast_fusion.5, f32[1,1,32,256]{3,2,1,0:T(8,128)S(1)} %convolution_bitcast_fusion.6, f32[1,1,32,256]{3,2,1,0:T(8,128)S(1)} %convolution_bitcast_fusion.7, ...), kind=kLoop, calls=%fused_computation.2492 | loop fusion | flops 108544 | bytes 229484 | tf_op jit(solution)/shard_map/stack | solution.py:129
  364.8 17.1 %fusion.1551 = f32[1,1,1,32,64]{4,3,2,1,0:T(8,128)S(1)} fusion(f32[1,1,32,256]{3,2,1,0:T(8,128)S(1)} %convolution_bitcast_fusion.4, f32[1,1,32,256]{3,2,1,0:T(8,128)S(1)} %convolution_bitcast_fusion.5, f32[1,1,32,256]{3,2,1,0:T(8,128)S(1)} %convolution_bitcast_fusion.6, f32[1,1,32,256]{3,2,1,0:T(8,128)S(1)} %convolution_bitcast_fusion.7, ...), kind=kLoop, calls=%fused_computation.2384 | loop fusion | flops 108544 | bytes 229484 | tf_op jit(solution)/shard_map/stack | solution.py:129
  381.9 16.9 %fusion.1524 = f32[1,1,1,32,64]{4,3,2,1,0:T(8,128)S(1)} fusion(f32[1,1,32,256]{3,2,1,0:T(8,128)S(1)} %convolution_bitcast_fusion.4, f32[1,1,32,256]{3,2,1,0:T(8,128)S(1)} %convolution_bitcast_fusion.5, f32[1,1,32,256]{3,2,1,0:T(8,128)S(1)} %convolution_bitcast_fusion.6, f32[1,1,32,256]{3,2,1,0:T(8,128)S(1)} %convolution_bitcast_fusion.7, ...), kind=kLoop, calls=%fused_computation.2330 | loop fusion | flops 108544 | bytes 229484 | tf_op jit(solution)/shard_map/stack | solution.py:129
  436.9 4.2 all_to_all.20
  545.0 4.4 fusion.1246
  549.4 26.5 %add_convert_fusion = bf16[16,16,32,256]{3,2,1,0:T(8,128)(2,1)} fusion(f32[16,16,32,256]{3,2,1,0:T(8,128)} %fusion.10, f32[16,16,32,256]{3,2,1,0:T(8,128)} %fusion.24, f32[16,16,32,256]{3,2,1,0:T(8,128)} %fusion.22, f32[16,16,32,256]{3,2,1,0:T(8,128)} %fusion.435, f32[16,16,32,256]{3,2,1,0:T(8,128)} %fusion.25, f32[16,16,32,256]{3,2,1,0:T(8,128)} %fusion.23, ...), kind=kOutput, calls=%fused_computation.36 | convolution fusion | flops 1106509824 | bytes 85721088 | tf_op jit(solution)/shard_map/ijvs,ts->ijvt/dot_general | solution.py:250
  (1138 shorter events, 314.8 us)
Async XLA Ops:
  0.0 109.5 %copy-start = (bf16[64,256]{1,0:T(8,128)(2,1)S(1)}, bf16[64,256]{1,0:T(8,128)(2,1)}, u32[]{:S(2)}) copy-start(bf16[64,256]{1,0:T(8,128)(2,1)} %param.10) | copy-start | bytes 98308
  2.4 80.3 %collective-permute-start = (bf16[2,16,32,256]{3,2,1,0:T(8,128)(2,1)}, bf16[2,16,32,256]{3,2,1,0:T(8,128)(2,1)S(1)}, u32[]{:S(2)}, u32[]{:S(2)}) collective-permute-start(bf16[2,16,32,256]{3,2,1,0:T(8,128)(2,1)} %get-tuple-element.334), channel_id=1, source_target_pairs={{0,16},{16,32},{32,48},{48,64},{64,80},{80,96},{96,112},{1,17},{17... | collective-permute-start | bytes 1572872 | tf_op jit(solution)/shard_map/ppermute | solution.py:17
  4.4 81.2 %collective-permute-start.1 = (bf16[2,16,32,256]{3,2,1,0:T(8,128)(2,1)}, bf16[2,16,32,256]{3,2,1,0:T(8,128)(2,1)S(1)}, u32[]{:S(2)}, u32[]{:S(2)}) collective-permute-start(bf16[2,16,32,256]{3,2,1,0:T(8,128)(2,1)} %get-tuple-element.335), channel_id=1, source_target_pairs={{16,0},{32,16},{48,32},{64,48},{80,64},{96,80},{112,96},{17,1},{33... | collective-permute-start | bytes 1572872 | tf_op jit(solution)/shard_map/ppermute | solution.py:20
  85.9 17.4 %collective-permute-start.3 = (bf16[20,2,32,256]{3,2,1,0:T(8,128)(2,1)S(1)}, bf16[20,2,32,256]{3,2,1,0:T(8,128)(2,1)S(1)}, u32[]{:S(2)}, u32[]{:S(2)}) collective-permute-start(bf16[20,2,32,256]{3,2,1,0:T(8,128)(2,1)S(1)} %get-tuple-element.332), channel_id=1, source_target_pairs={{1,0},{2,1},{3,2},{4,3},{5,4},{6,5},{7,6},{8,7},{9,8},{10,9},{11,1... | collective-permute-start | bytes 1966088 | tf_op jit(solution)/shard_map/ppermute | solution.py:20
  90.3 19.2 %collective-permute-start.2 = (bf16[20,2,32,256]{3,2,1,0:T(8,128)(2,1)S(1)}, bf16[20,2,32,256]{3,2,1,0:T(8,128)(2,1)S(1)}, u32[]{:S(2)}, u32[]{:S(2)}) collective-permute-start(bf16[20,2,32,256]{3,2,1,0:T(8,128)(2,1)S(1)} %get-tuple-element.333), channel_id=1, source_target_pairs={{0,1},{1,2},{2,3},{3,4},{4,5},{5,6},{6,7},{7,8},{8,9},{9,10},{10,1... | collective-permute-start | bytes 1966088 | tf_op jit(solution)/shard_map/ppermute | solution.py:17
  177.4 132.1 %collective-permute-start.4 = (bf16[2,8,2048]{2,1,0:T(8,128)(2,1)}, bf16[2,8,2048]{2,1,0:T(8,128)(2,1)}, u32[]{:S(2)}, u32[]{:S(2)}) collective-permute-start(bf16[2,8,2048]{2,1,0:T(8,128)(2,1)} %slice.5004), channel_id=1, source_target_pairs={{0,16},{16,32},{32,48},{48,64},{64,80},{80,96},{96,112},{1,17},{17... | collective-permute-start | bytes 196616 | tf_op jit(solution)/shard_map/ppermute | solution.py:17
  185.6 104.9 %collective-permute-start.12 = (bf16[2,2,2048]{2,1,0:T(2,128)(2,1)}, bf16[2,2,2048]{2,1,0:T(2,128)(2,1)}, u32[]{:S(2)}, u32[]{:S(2)}) collective-permute-start(bf16[2,2,2048]{2,1,0:T(2,128)(2,1)} %reshape.1634), channel_id=1, source_target_pairs={{0,16},{16,32},{32,48},{48,64},{64,80},{80,96},{96,112},{1,17},{17... | collective-permute-start | bytes 49160 | tf_op jit(solution)/shard_map/ppermute | solution.py:17
  190.4 93.6 %all-to-all-start = ((bf16[4,2,1024]{2,1,0:T(2,128)(2,1)}), bf16[4,2,1024]{2,1,0:T(2,128)(2,1)S(1)}, u32[]{:S(2)}, u32[]{:S(2)}) async-start(bf16[4,2,1024]{2,1,0:T(2,128)(2,1)} %reshape.2124), calls=%async_computation | async-start | bytes 32768 | tf_op jit(solution)/shard_map/all_to_all | solution.py:35
  198.9 97.5 %collective-permute-start.8 = (bf16[2,4,2048]{2,1,0:T(4,128)(2,1)}, bf16[2,4,2048]{2,1,0:T(4,128)(2,1)}, u32[]{:S(2)}, u32[]{:S(2)}) collective-permute-start(bf16[2,4,2048]{2,1,0:T(4,128)(2,1)} %slice.5302), channel_id=1, source_target_pairs={{0,16},{16,32},{32,48},{48,64},{64,80},{80,96},{96,112},{1,17},{17... | collective-permute-start | bytes 98312 | tf_op jit(solution)/shard_map/ppermute | solution.py:17
  278.0 16.4 %collective-permute-start.13 = (bf16[2,2,2048]{2,1,0:T(2,128)(2,1)}, bf16[2,2,2048]{2,1,0:T(2,128)(2,1)S(1)}, u32[]{:S(2)}, u32[]{:S(2)}) collective-permute-start(bf16[2,2,2048]{2,1,0:T(2,128)(2,1)} %reshape.1634), channel_id=1, source_target_pairs={{16,0},{32,16},{48,32},{64,48},{80,64},{96,80},{112,96},{17,1},{33... | collective-permute-start | bytes 49160 | tf_op jit(solution)/shard_map/ppermute | solution.py:20
  281.9 33.9 %collective-permute-start.5 = (bf16[2,8,2048]{2,1,0:T(8,128)(2,1)S(1)}, bf16[2,8,2048]{2,1,0:T(8,128)(2,1)S(1)}, u32[]{:S(2)}, u32[]{:S(2)}) collective-permute-start(bf16[2,8,2048]{2,1,0:T(8,128)(2,1)S(1)} %slice.5006), channel_id=1, source_target_pairs={{16,0},{32,16},{48,32},{64,48},{80,64},{96,80},{112,96},{17,1},{33... | collective-permute-start | bytes 196616 | tf_op jit(solution)/shard_map/ppermute | solution.py:20
  284.8 18.5 %all-to-all-start.1 = ((bf16[4,4,1,2048]{3,1,2,0:T(4,128)(2,1)}), bf16[4,4,1,2048]{3,1,2,0:T(4,128)(2,1)S(1)}, u32[]{:S(2)}, u32[]{:S(2)}) async-start(bf16[4,4,1,2048]{3,1,2,0:T(4,128)(2,1)} %stack.157), calls=%async_computation.1 | async-start | bytes 131072 | tf_op jit(solution)/shard_map/all_to_all | solution.py:35
  290.5 10.6 %collective-permute-start.9 = (bf16[2,4,2048]{2,1,0:T(4,128)(2,1)S(1)}, bf16[2,4,2048]{2,1,0:T(4,128)(2,1)S(1)}, u32[]{:S(2)}, u32[]{:S(2)}) collective-permute-start(bf16[2,4,2048]{2,1,0:T(4,128)(2,1)S(1)} %slice.5304), channel_id=1, source_target_pairs={{16,0},{32,16},{48,32},{64,48},{80,64},{96,80},{112,96},{17,1},{33... | collective-permute-start | bytes 98312 | tf_op jit(solution)/shard_map/ppermute | solution.py:20
  294.4 24.2 %collective-permute-start.15 = (bf16[6,2,2048]{2,1,0:T(2,128)(2,1)S(1)}, bf16[6,2,2048]{2,1,0:T(2,128)(2,1)S(1)}, u32[]{:S(2)}, u32[]{:S(2)}) collective-permute-start(bf16[6,2,2048]{2,1,0:T(2,128)(2,1)S(1)} %constant_dynamic-update-slice_fusion.9), channel_id=1, source_target_pairs={{1,0},{2,1},{3,2},{4,3},{5,4},{6,5},{7,6},{8,7},{9,8},{10,9},{11,1... | collective-permute-start | bytes 147464 | tf_op jit(solution)/shard_map/ppermute | solution.py:20
  296.4 28.5 %collective-permute-start.14 = (bf16[6,2,2048]{2,1,0:T(2,128)(2,1)S(1)}, bf16[6,2,2048]{2,1,0:T(2,128)(2,1)S(1)}, u32[]{:S(2)}, u32[]{:S(2)}) collective-permute-start(bf16[6,2,2048]{2,1,0:T(2,128)(2,1)S(1)} %constant_dynamic-update-slice_fusion.9), channel_id=1, source_target_pairs={{0,1},{1,2},{2,3},{3,4},{4,5},{5,6},{6,7},{7,8},{8,9},{9,10},{10,1... | collective-permute-start | bytes 147464 | tf_op jit(solution)/shard_map/ppermute | solution.py:17
  301.3 98.1 %collective-permute-start.10 = (bf16[8,2,2048]{2,1,0:T(2,128)(2,1)S(1)}, bf16[8,2,2048]{2,1,0:T(2,128)(2,1)S(1)}, u32[]{:S(2)}, u32[]{:S(2)}) collective-permute-start(bf16[8,2,2048]{2,1,0:T(2,128)(2,1)S(1)} %get-tuple-element.509), channel_id=1, source_target_pairs={{0,1},{1,2},{2,3},{3,4},{4,5},{5,6},{6,7},{7,8},{8,9},{9,10},{10,1... | collective-permute-start | bytes 196616 | tf_op jit(solution)/shard_map/ppermute | solution.py:17
  304.0 132.8 %all-to-all-start.2 = ((bf16[4,16,1,2048]{3,1,2,0:T(8,128)(2,1)}), bf16[4,16,1,2048]{3,1,2,0:T(8,128)(2,1)S(1)}, u32[]{:S(2)}, u32[]{:S(2)}) async-start(bf16[4,16,1,2048]{3,1,2,0:T(8,128)(2,1)} %stack.158), calls=%async_computation.2 | async-start | bytes 524288 | tf_op jit(solution)/shard_map/all_to_all | solution.py:35
  309.5 89.9 %collective-permute-start.11 = (bf16[8,2,2048]{2,1,0:T(2,128)(2,1)S(1)}, bf16[8,2,2048]{2,1,0:T(2,128)(2,1)S(1)}, u32[]{:S(2)}, u32[]{:S(2)}) collective-permute-start(bf16[8,2,2048]{2,1,0:T(2,128)(2,1)S(1)} %get-tuple-element.510), channel_id=1, source_target_pairs={{1,0},{2,1},{3,2},{4,3},{5,4},{6,5},{7,6},{8,7},{9,8},{10,9},{11,1... | collective-permute-start | bytes 196616 | tf_op jit(solution)/shard_map/ppermute | solution.py:20
  316.6 96.0 %collective-permute-start.6 = (bf16[12,2,2048]{2,1,0:T(2,128)(2,1)}, bf16[12,2,2048]{2,1,0:T(2,128)(2,1)}, u32[]{:S(2)}, u32[]{:S(2)}) collective-permute-start(bf16[12,2,2048]{2,1,0:T(2,128)(2,1)} %get-tuple-element.503), channel_id=1, source_target_pairs={{0,1},{1,2},{2,3},{3,4},{4,5},{5,6},{6,7},{7,8},{8,9},{9,10},{10,1... | collective-permute-start | bytes 294920 | tf_op jit(solution)/shard_map/ppermute | solution.py:17
  318.6 94.0 %collective-permute-start.7 = (bf16[12,2,2048]{2,1,0:T(2,128)(2,1)}, bf16[12,2,2048]{2,1,0:T(2,128)(2,1)}, u32[]{:S(2)}, u32[]{:S(2)}) collective-permute-start(bf16[12,2,2048]{2,1,0:T(2,128)(2,1)} %get-tuple-element.504), channel_id=1, source_target_pairs={{1,0},{2,1},{3,2},{4,3},{5,4},{6,5},{7,6},{8,7},{9,8},{10,9},{11,1... | collective-permute-start | bytes 294920 | tf_op jit(solution)/shard_map/ppermute | solution.py:20
  330.2 70.0 %copy-start.41 = (bf16[64,64]{0,1:T(8,128)(2,1)S(1)}, bf16[64,64]{0,1:T(8,128)(2,1)}, u32[]{:S(2)}) copy-start(bf16[64,64]{0,1:T(8,128)(2,1)} %get-tuple-element.414) | copy-start | bytes 24580
  330.2 70.0 %copy-start.42 = (bf16[64,64]{0,1:T(8,128)(2,1)S(1)}, bf16[64,64]{0,1:T(8,128)(2,1)}, u32[]{:S(2)}) copy-start(bf16[64,64]{0,1:T(8,128)(2,1)} %get-tuple-element.416) | copy-start | bytes 24580
  330.4 70.1 %copy-start.43 = (bf16[64,64]{0,1:T(8,128)(2,1)S(1)}, bf16[64,64]{0,1:T(8,128)(2,1)}, u32[]{:S(2)}) copy-start(bf16[64,64]{0,1:T(8,128)(2,1)} %get-tuple-element.418) | copy-start | bytes 24580
  330.4 70.3 %copy-start.45 = (bf16[64,64]{0,1:T(8,128)(2,1)S(1)}, bf16[64,64]{0,1:T(8,128)(2,1)}, u32[]{:S(2)}) copy-start(bf16[64,64]{0,1:T(8,128)(2,1)} %get-tuple-element.404) | copy-start | bytes 24580
  330.4 70.3 %copy-start.47 = (bf16[64,64]{0,1:T(8,128)(2,1)S(1)}, bf16[64,64]{0,1:T(8,128)(2,1)}, u32[]{:S(2)}) copy-start(bf16[64,64]{0,1:T(8,128)(2,1)} %get-tuple-element.399) | copy-start | bytes 24580
  330.5 70.3 %copy-start.44 = (bf16[64,64]{0,1:T(8,128)(2,1)S(1)}, bf16[64,64]{0,1:T(8,128)(2,1)}, u32[]{:S(2)}) copy-start(bf16[64,64]{0,1:T(8,128)(2,1)} %get-tuple-element.408) | copy-start | bytes 24580
  330.5 70.5 %copy-start.49 = (bf16[64,64]{0,1:T(8,128)(2,1)S(1)}, bf16[64,64]{0,1:T(8,128)(2,1)}, u32[]{:S(2)}) copy-start(bf16[64,64]{0,1:T(8,128)(2,1)} %get-tuple-element.392) | copy-start | bytes 24580
  330.5 70.6 %copy-start.50 = (bf16[64,64]{0,1:T(8,128)(2,1)S(1)}, bf16[64,64]{0,1:T(8,128)(2,1)}, u32[]{:S(2)}) copy-start(bf16[64,64]{0,1:T(8,128)(2,1)} %get-tuple-element.391) | copy-start | bytes 24580
  330.5 70.7 %copy-start.48 = (bf16[64,64]{0,1:T(8,128)(2,1)S(1)}, bf16[64,64]{0,1:T(8,128)(2,1)}, u32[]{:S(2)}) copy-start(bf16[64,64]{0,1:T(8,128)(2,1)} %get-tuple-element.393) | copy-start | bytes 24580
  347.0 54.7 %copy-start.39 = (bf16[64,64]{0,1:T(8,128)(2,1)S(1)}, bf16[64,64]{0,1:T(8,128)(2,1)}, u32[]{:S(2)}) copy-start(bf16[64,64]{0,1:T(8,128)(2,1)} %get-tuple-element.406) | copy-start | bytes 24580
  347.0 55.1 %copy-start.96 = (bf16[64,64]{0,1:T(8,128)(2,1)S(1)}, bf16[64,64]{0,1:T(8,128)(2,1)}, u32[]{:S(2)}) copy-start(bf16[64,64]{0,1:T(8,128)(2,1)} %get-tuple-element.383) | copy-start | bytes 24580
  347.1 55.1 %copy-start.102 = (bf16[64,64]{0,1:T(8,128)(2,1)S(1)}, bf16[64,64]{0,1:T(8,128)(2,1)}, u32[]{:S(2)}) copy-start(bf16[64,64]{0,1:T(8,128)(2,1)} %get-tuple-element.384) | copy-start | bytes 24580
  (341 other events, 2861.2 us)
